TPU v7x, 32 devices: a whole 2x2x4 slice. The times are simulated.
32 devices in a mesh: groups: 1, tensor: 32 (over z, y, x, core).
Axes of the slice: x: 2, y: 2, z: 4, core: 2. Of those that a mesh axis runs over, the one named last changes fastest.
Arguments:
- hidden_in: bfloat16 [4, 16384], P('groups', 'tensor'), may hold values from -0.59765625 to 0.59765625
- norm_gain: bfloat16 [16384], P('tensor'), may hold values from 0.5 to 1.5
- w_q: bfloat16 [16384, 16384], P('tensor'), may hold values from -1 to 256
- w_kv: bfloat16 [16384, 2048], P('tensor'), may hold values from -0.046875 to 0.046875
- w_o: bfloat16 [16384, 16384], P(None, 'tensor'), may hold values from -0.046875 to 0.046875
- kv_cache: bfloat16 [8, 4, 2, 4096, 128], P(None, 'groups', None, 'tensor'), may hold values from -8 to 8
- lengths: int32 [4], P('groups'), may hold values from 2 to 4096, as said below
- slab_index: int32 [8, 4], P(None, 'groups'), may hold values from 0 to 3, each once within a row
Outputs:
- hidden_out: bfloat16 [4, 16384], P('groups', 'tensor')
Inputs may be any that keep to these rules, and one draw needn't show every extreme that they name: `lengths`: one request in every draw has exactly 4096 cached tokens.
All inputs are finite; a program needn't handle non-finite values.
Results may differ from a plain program's by a relative error of at most 0.0085.
The roundings to bfloat16 on the way count: a program that leaves them out, or rounds other values in their place, can miss the bound.
Values may be sent and summed in bfloat16 or wider, within the bound.
A program may use at most 128 MiB of HBM per device.

v0:
```python
import functools

import jax
import jax.numpy as jnp
from jax import lax
from jax.experimental import pallas as pl
from jax.experimental.pallas import tpu as pltpu
from jax.sharding import PartitionSpec as P

KVH = 8
HD = 128
GROUP = 16

epsilon = 1e-05
rope_base = 500000.0
score_scale = 1.0 / HD**0.5
lowest = -1e30


def step_kernel(
    n,
    slab_ref,
    len_ref,
    hidden_ref,
    gain_ref,
    cos_ref,
    sin_ref,
    wq_hbm,
    wkv_hbm,
    wo_hbm,
    kv_hbm,
    out_ref,
    wq_v,
    wkv_v,
    wo_v,
    kv_v,
    sq_buf,
    kvp,
    part_buf,
    part_in,
    q_buf,
    fin,
    k_rows,
    v_rows,
    o_buf,
    o_in,
    st_buf,
    st_in,
    att_f,
    att_buf,
    wq_sem,
    wkv_sem,
    wo_sem,
    kv_sem,
    send_sem,
    recv_sem,
    att_sem,
):
    me = lax.axis_index("tensor")
    requests, width = hidden_ref.shape
    heads = KVH * GROUP // n
    cols = heads * HD
    q_rows = heads * requests
    per_kv = GROUP // heads
    slabs, positions = kv_v.shape[1], kv_v.shape[3]

    def wq_copy(step):
        owner = lax.rem(me + 1 + step, n)
        return pltpu.make_async_copy(
            wq_hbm.at[:, pl.ds(pl.multiple_of(owner * cols, cols), cols)],
            wq_v.at[step],
            wq_sem.at[step],
        )

    wkv_copy = pltpu.make_async_copy(wkv_hbm, wkv_v, wkv_sem)
    wo_copy = pltpu.make_async_copy(wo_hbm, wo_v, wo_sem)
    kv_copy = pltpu.make_async_copy(kv_hbm, kv_v, kv_sem)
    wkv_copy.start()

    @pl.loop(0, n)
    def _(step):
        wq_copy(step).start()

    def remote(src, dst, phase, peer):
        return pltpu.make_async_remote_copy(
            src_ref=src,
            dst_ref=dst,
            send_sem=send_sem.at[phase],
            recv_sem=recv_sem.at[phase],
            device_id={"tensor": peer},
            device_id_type=pl.DeviceIdType.MESH,
        )

    def wait_all(buf, phase, sent=True, received=True):
        every = buf.at[pl.ds(0, n - 1)]
        descriptor = remote(every, every, phase, lax.rem(me + 1, n))
        if received:
            descriptor.wait_recv()
        if sent:
            descriptor.wait_send()

    barrier = pltpu.get_barrier_semaphore()

    @pl.loop(1, n)
    def _(step):
        pl.semaphore_signal(
            barrier,
            inc=1,
            device_id={"tensor": lax.rem(me + step, n)},
            device_id_type=pl.DeviceIdType.MESH,
        )

    stream = hidden_ref[...].astype(jnp.float32)
    own_sq = jnp.sum(stream * stream, axis=1, keepdims=True)
    sq_buf[me] = jnp.broadcast_to(own_sq, (requests, HD))
    pl.semaphore_wait(barrier, n - 1)

    @pl.loop(1, n)
    def _(step):
        remote(sq_buf.at[me], sq_buf.at[me], 0, lax.rem(me + step, n)).start()

    wait_all(sq_buf, 0)
    squares = jnp.sum(sq_buf[...], axis=0)[:, :1]
    normed = (
        stream
        * lax.rsqrt(squares / (width * n) + epsilon)
        * gain_ref[...].astype(jnp.float32)
    ).astype(jnp.bfloat16)

    wkv_copy.wait()
    for piece in range(2 * KVH * HD // 512):
        res = jnp.dot(
            normed, wkv_v[:, piece * 512 : (piece + 1) * 512], preferred_element_type=jnp.float32
        )
        for j in range(4):
            kvp[piece * 4 + j] = res[:, j * HD : (j + 1) * HD]

    def project(step, target):
        owner = lax.rem(me + 1 + step, n)
        wq_copy(step).wait()
        res = jnp.dot(normed, wq_v[step], preferred_element_type=jnp.float32)
        for j in range(heads):
            target[j * requests : (j + 1) * requests, :] = res[:, j * HD : (j + 1) * HD]
        kv_head = owner // per_kv
        target[q_rows : q_rows + requests, :] = kvp[kv_head]
        target[q_rows + requests : q_rows + 2 * requests, :] = kvp[KVH + kv_head]
        return owner

    @pl.loop(0, n - 1, unroll=True)
    def _(step):
        owner = project(step, part_buf.at[step])
        remote(part_buf.at[step], part_in.at[me], 1, owner).start()

    kv_copy.start()
    wo_copy.start()
    project(n - 1, part_in.at[me])
    wait_all(part_in, 1)

    total = jnp.sum(part_in[...], axis=0)
    total = total * cos_ref[...] + pltpu.roll(total, HD // 2, 1) * sin_ref[...]
    rounded = total.astype(jnp.bfloat16)
    fin[...] = rounded.astype(jnp.float32)
    q_buf[me] = fin[:q_rows, :].astype(jnp.bfloat16)

    @pl.loop(1, n)
    def _(step):
        remote(q_buf.at[me], q_buf.at[me], 2, lax.rem(me + step, n)).start()

    for j in range(heads):
        k_rows[j * requests : (j + 1) * requests, :] = fin[q_rows : q_rows + requests, :]
        v_rows[j * requests : (j + 1) * requests, :] = fin[
            q_rows + requests : q_rows + 2 * requests, :
        ]
    new_score = jnp.sum(fin[:q_rows, :] * k_rows[...], axis=1, keepdims=True) * score_scale
    lane = lax.broadcasted_iota(jnp.int32, (q_rows, HD), 1)
    row = lax.broadcasted_iota(jnp.int32, (q_rows, HD), 0)
    diagonal = lane == row
    shifted = lane == row + HD // 2
    new_lane = jnp.sum(jnp.where(diagonal, new_score, 0.0), axis=0, keepdims=True)

    all_rows = GROUP * requests
    keys = slabs * positions
    row_req = lax.rem(lax.broadcasted_iota(jnp.int32, (all_rows, 1), 0), requests)
    column = lax.broadcasted_iota(jnp.int32, (1, keys), 1)
    column_slab = column // positions
    column_pos = lax.rem(column, positions) + me * positions
    row_len = jnp.zeros((all_rows, 1), jnp.int32)
    for b in range(requests):
        row_len = jnp.where(row_req == b, len_ref[b], row_len)
    in_length = column_pos < row_len

    kv_copy.wait()
    wait_all(q_buf, 2)

    @pl.loop(0, KVH, unroll=True)
    def _(h):
        row_slab = jnp.zeros((all_rows, 1), jnp.int32)
        for b in range(requests):
            row_slab = jnp.where(row_req == b, slab_ref[h, b], row_slab)
        visible = jnp.logical_and(column_slab == row_slab, in_length)
        queries = q_buf[pl.ds(h * per_kv, per_kv)].reshape(all_rows, HD)
        key_block = kv_v[h, :, 0].reshape(keys, HD)
        value_block = kv_v[h, :, 1].reshape(keys, HD)
        scores = (
            lax.dot_general(
                queries, key_block, (((1,), (1,)), ((), ())), preferred_element_type=jnp.float32
            )
            * score_scale
        )
        scores = jnp.where(visible, scores, lowest)
        top = jnp.max(scores, axis=1, keepdims=True)
        weights = jnp.where(visible, jnp.exp(scores - top), 0.0)
        weight_sum = jnp.sum(weights, axis=1, keepdims=True)
        weighted = jnp.dot(
            weights.astype(jnp.bfloat16), value_block, preferred_element_type=jnp.float32
        )
        for t in range(per_kv):
            owner = h * per_kv + t
            own = slice(t * q_rows, (t + 1) * q_rows)
            o_buf[owner] = weighted[own].astype(jnp.bfloat16)
            st_buf[owner] = jnp.sum(
                jnp.where(diagonal, top[own], 0.0) + jnp.where(shifted, weight_sum[own], 0.0),
                axis=0,
                keepdims=True,
            )

    o_in[me] = o_buf[me]
    st_in[me] = st_buf[me]

    @pl.loop(1, n)
    def _(step):
        peer = lax.rem(me + step, n)
        remote(st_buf.at[peer], st_in.at[me], 3, peer).start()
        remote(o_buf.at[peer], o_in.at[me], 4, peer).start()

    wait_all(st_in, 3)
    stats = st_in[...]
    top_lane = jnp.maximum(jnp.max(stats, axis=0), new_lane)
    factor = jnp.exp(jnp.minimum(stats - top_lane[None], 0.0))
    new_factor = jnp.exp(new_lane - top_lane)
    sums = jnp.concatenate([stats[:, :, HD // 2 :], stats[:, :, : HD // 2]], axis=2)
    denominator_lane = jnp.sum(factor * sums, axis=0) + new_factor

    def as_column(lanes):
        return jnp.sum(jnp.where(diagonal, lanes, 0.0), axis=1, keepdims=True)

    wait_all(o_in, 4)
    weighted = as_column(new_factor).astype(jnp.bfloat16).astype(jnp.float32) * v_rows[...]
    columns = jnp.sum(jnp.where(diagonal[None], factor, 0.0), axis=2, keepdims=True)
    weighted = weighted + jnp.sum(columns * o_in[...].astype(jnp.float32), axis=0)
    att_f[...] = weighted / as_column(denominator_lane)
    for j in range(heads):
        att_buf[me, :, j * HD : (j + 1) * HD] = att_f[
            j * requests : (j + 1) * requests, :
        ].astype(jnp.bfloat16)

    def att_copy(peer, source):
        return pltpu.make_async_remote_copy(
            src_ref=att_buf.at[source],
            dst_ref=att_buf.at[source],
            send_sem=send_sem.at[5],
            recv_sem=att_sem.at[source],
            device_id={"tensor": peer},
            device_id_type=pl.DeviceIdType.MESH,
        )

    @pl.loop(1, n)
    def _(step):
        att_copy(lax.rem(me + step, n), me).start()

    wo_copy.wait()

    def project_out(source):
        return jnp.dot(
            att_buf[source],
            wo_v[pl.ds(pl.multiple_of(source * cols, cols), cols), :],
            preferred_element_type=jnp.float32,
        )

    def add(step, acc):
        source = lax.rem(me + n - step, n)
        att_copy(lax.rem(me + 1, n), source).wait_recv()
        return acc + project_out(source)

    acc = lax.fori_loop(1, n, add, project_out(me))
    out_ref[...] = (stream + acc).astype(jnp.bfloat16)
    wait_all(att_buf, 5, received=False)


def body(n, hidden_in, norm_gain, w_q, w_kv, w_o, kv_cache, lengths, slab_index):
    requests, width = hidden_in.shape
    heads = KVH * GROUP // n
    cols = heads * HD
    q_rows = heads * requests
    all_rows = q_rows + 2 * requests
    slabs, positions = kv_cache.shape[1], kv_cache.shape[3]

    half = HD // 2
    frequency = rope_base ** (-2.0 * jnp.arange(half, dtype=jnp.float32) / HD)
    angles = lengths.astype(jnp.float32)[:, None] * frequency
    cosine, sine = jnp.cos(angles), jnp.sin(angles)
    cosine = jnp.concatenate([cosine, cosine], axis=1)
    sine = jnp.concatenate([-sine, sine], axis=1)
    cosine = jnp.concatenate([jnp.tile(cosine, (heads + 1, 1)), jnp.ones_like(cosine)], axis=0)
    sine = jnp.concatenate([jnp.tile(sine, (heads + 1, 1)), jnp.zeros_like(sine)], axis=0)

    vmem = pl.BlockSpec(memory_space=pltpu.VMEM)
    smem = pl.BlockSpec(memory_space=pltpu.SMEM)
    hbm = pl.BlockSpec(memory_space=pl.ANY)
    bf16, f32 = jnp.bfloat16, jnp.float32
    return pl.pallas_call(
        functools.partial(step_kernel, n),
        out_shape=jax.ShapeDtypeStruct((requests, width), bf16),
        in_specs=[smem, smem, vmem, vmem, vmem, vmem, hbm, hbm, hbm, hbm],
        out_specs=vmem,
        scratch_shapes=[
            pltpu.VMEM((n, width, cols), bf16),
            pltpu.VMEM(w_kv.shape, bf16),
            pltpu.VMEM(w_o.shape, bf16),
            pltpu.VMEM(kv_cache.shape, bf16),
            pltpu.VMEM((n, requests, HD), f32),
            pltpu.VMEM((2 * KVH, requests, HD), f32),
            pltpu.VMEM((n - 1, all_rows, HD), f32),
            pltpu.VMEM((n, all_rows, HD), f32),
            pltpu.VMEM((n, q_rows, HD), bf16),
            pltpu.VMEM((all_rows, HD), f32),
            pltpu.VMEM((q_rows, HD), f32),
            pltpu.VMEM((q_rows, HD), f32),
            pltpu.VMEM((n, q_rows, HD), bf16),
            pltpu.VMEM((n, q_rows, HD), bf16),
            pltpu.VMEM((n, 1, HD), f32),
            pltpu.VMEM((n, 1, HD), f32),
            pltpu.VMEM((q_rows, HD), f32),
            pltpu.VMEM((n, requests, cols), bf16),
            pltpu.SemaphoreType.DMA((n,)),
            pltpu.SemaphoreType.DMA,
            pltpu.SemaphoreType.DMA,
            pltpu.SemaphoreType.DMA,
            pltpu.SemaphoreType.DMA((6,)),
            pltpu.SemaphoreType.DMA((5,)),
            pltpu.SemaphoreType.DMA((n,)),
        ],
        compiler_params=pltpu.CompilerParams(
            collective_id=0, has_side_effects=True, vmem_limit_bytes=56 * 1024 * 1024
        ),
    )(
        slab_index,
        lengths,
        hidden_in,
        norm_gain.reshape(1, width),
        cosine,
        sine,
        w_q,
        w_kv,
        w_o,
        kv_cache,
    )


def solution(mesh):
    placed = (
        P("groups", "tensor"),
        P("tensor"),
        P("tensor", None),
        P("tensor", None),
        P(None, "tensor"),
        P(None, "groups", None, "tensor", None),
        P("groups"),
        P(None, "groups"),
    )
    return jax.shard_map(
        functools.partial(body, mesh.shape["tensor"]),
        mesh=mesh,
        in_specs=placed,
        out_specs=P("groups", "tensor"),
        check_vma=False,
    )
```

profile of v0, /device:TPU:0, one launch (start us, length us, event | category | flops | bytes accessed | tf_op | source)
XLA Modules:
  0.0 55.7 jit_solution(4582487716170893653)
XLA Ops:
  0.0 0.7 %convert_element_type.3 = f32[4]{0:T(128)S(1)} convert(s32[4]{0:T(128)} %len_ref.1) | non-fusion elementwise | flops 4 | bytes 32 | tf_op jit(solution)/shard_map/convert_element_type | solution.py:300
  0.7 0.1 fusion
  0.8 0.1 pad_maximum_fusion
  0.9 0.6 %concatenate.13.cos_ref = f32[24,128]{1,0:T(8,128)} pad(f32[20,128]{1,0:T(8,128)S(1)} %tile.9, f32[]{:T(128)} %constant.3.clone.1), padding=0_4x0_0 | pad | bytes 22532 | tf_op jit(solution)/shard_map/concatenate | solution.py:304
  1.5 0.6 %concatenate.15.sin_ref = f32[24,128]{1,0:T(8,128)} pad(f32[20,128]{1,0:T(8,128)S(1)} %tile.21, f32[]{:T(128)} %constant.10.clone.1), padding=0_4x0_0 | pad | bytes 22532 | tf_op jit(solution)/shard_map/concatenate | solution.py:305
  2.1 1.3 %copy.9.slab_ref = s32[8,4]{1,0:T(8,128)} copy(s32[8,4]{0,1:T(4,128)} %param.15) | data formatting | bytes 256 | tf_op args[7]
  3.5 1.3 %reshape.17.gain_ref = bf16[1,512]{1,0:T(2,128)(2,1)} reshape(bf16[512]{0:T(512)(128)(2,1)} %param.9) | data formatting | bytes 2048 | tf_op jit(solution)/shard_map/reshape | solution.py:350
  4.7 49.7 %shard_map.82 = bf16[4,512]{1,0:T(4,128)(2,1)} custom-call(s32[8,4]{1,0:T(8,128)} %copy.9.slab_ref, s32[4]{0:T(128)} %len_ref.1, bf16[4,512]{1,0:T(4,128)(2,1)} %hidden_ref.1, bf16[1,512]{1,0:T(2,128)(2,1)} %reshape.17.gain_ref, f32[24,128]{1,0:T(8,128)} %concatenate.13.cos_ref, f32[24,128]{1,0:T(8,128)} %concatenate.15.sin_ref, bf16[512,16384]{1,0:T(8,128)(2,1)} %wq_hbm.1, ...), custom_call_target="tpu_custom_call" | custom-call | tf_op jit(solution)/shard_map/pallas_call | solution.py:311
  54.5 1.3 %copy.11 = bf16[4,512]{1,0:T(4,128)(2,1)} copy(bf16[4,512]{1,0:T(4,128)(2,1)} %shard_map.82) | data formatting | bytes 8192
  (5 shorter events, 0.0 us)
where the time goes:
time: 56 us; the launch traced here: 55.7 us
  Pallas kernels  49.7 us (89%)
  local copies, waits for them, and re-layouts  5.12 us (9%)
  other arithmetic  0.85 us (2%)
    pallas_call x1, Pallas kernels, body(): pl.pallas_call(functools.partial(step_kernel, n), out_shape=jax.ShapeDtyp...  49.7 us
    unnamed x2, local copies, waits for them, and re-layouts  2.62 us
    reshape x1, local copies, waits for them, and re-layouts, body(): norm_gain.reshape(1, width)  1.26 us

commit v1 on v0

v1 whole, which is shorter than its diff:
```python
import functools

import jax
import jax.numpy as jnp
import numpy as np
from jax import lax
from jax.experimental import pallas as pl
from jax.experimental.pallas import tpu as pltpu
from jax.sharding import PartitionSpec as P

KVH = 8
HD = 128
GROUP = 16

epsilon = 1e-05
rope_base = 500000.0
score_scale = 1.0 / HD**0.5
lowest = -1e30
STAGES = 4


def step_kernel(
    n,
    slab_hbm,
    len_hbm,
    hidden_hbm,
    gain_hbm,
    freq_hbm,
    wq_hbm,
    wkv_hbm,
    wo_hbm,
    kv_hbm,
    out_ref,
    slab_ref,
    len_ref,
    hidden_v,
    gain_v,
    freq_v,
    wq_v,
    wkv_v,
    wo_v,
    kv_v,
    sq_buf,
    kvp,
    kv_d,
    kv_sum,
    kv_in,
    kv_sib,
    kv_flat,
    q_other,
    q_own,
    q_d,
    q_in,
    q_buf,
    k_rows,
    v_rows,
    o_buf,
    o_in,
    st_buf,
    st_in,
    att_f,
    att_buf,
    small_sem,
    wq_sem,
    wkv_sem,
    wo_sem,
    kv_sem,
    send_sem,
    recv_sem,
    pair_sem,
    att_sem,
):
    me = lax.axis_index("tensor")
    requests, width = hidden_hbm.shape
    chips = n // 2
    chip, core = me // 2, lax.rem(me, 2)
    partner = chip * 2 + 1 - core
    heads = KVH * GROUP // n
    cols = heads * HD
    q_rows = heads * requests
    per_kv = GROUP // heads
    half_kv = KVH // 2
    kv_rows = 2 * requests // per_kv
    slabs, positions = kv_hbm.shape[1], kv_hbm.shape[3]
    span = 2 * positions
    in_stage = chips // STAGES

    flips = []
    bit = 1
    while bit < n:
        flips.append(bit * (1 - 2 * lax.rem(me // bit, 2)))
        bit *= 2

    def flipped(mask):
        peer = me
        for k, flip in enumerate(flips):
            if mask >> k & 1:
                peer = peer + flip
        return peer

    def block_of(device):
        return lax.rem(device, 2) * chips + device // 2

    far_first = list(range(n - 1, 0, -1))
    chip_order = list(range(chips - 1, -1, -1))

    barrier = pltpu.get_barrier_semaphore()
    for mask in far_first:
        pl.semaphore_signal(
            barrier,
            inc=1,
            device_id={"tensor": flipped(mask)},
            device_id_type=pl.DeviceIdType.MESH,
        )

    small = [
        pltpu.make_async_copy(src, dst, small_sem.at[k])
        for k, (src, dst) in enumerate(
            (
                (hidden_hbm, hidden_v),
                (gain_hbm, gain_v),
                (len_hbm, len_ref),
                (freq_hbm, freq_v),
                (slab_hbm, slab_ref),
            )
        )
    ]
    for copy in small:
        copy.start()

    def wq_copy(block, slot):
        return pltpu.make_async_copy(
            wq_hbm.at[:, pl.ds(pl.multiple_of(block * cols, cols), cols)],
            wq_v.at[slot],
            wq_sem.at[slot],
        )

    wkv_copy = pltpu.make_async_copy(wkv_hbm, wkv_v, wkv_sem)
    wo_copy = pltpu.make_async_copy(wo_hbm, wo_v, wo_sem)
    wkv_copy.start()
    wq_copies = []
    for step, mask in enumerate(chip_order):
        device = flipped(2 * mask)
        target = device // 2
        wq_copies.append(wq_copy((1 - core) * chips + target, 2 * step))
        wq_copies.append(wq_copy(core * chips + target, 2 * step + 1))
    for copy in wq_copies:
        copy.start()

    def remote(src, dst, sent, received, peer):
        return pltpu.make_async_remote_copy(
            src_ref=src,
            dst_ref=dst,
            send_sem=sent,
            recv_sem=received,
            device_id={"tensor": peer},
            device_id_type=pl.DeviceIdType.MESH,
        )

    def every(buf, phase, count):
        part = buf.at[pl.ds(0, count)]
        return remote(part, part, send_sem.at[phase], recv_sem.at[phase], partner)

    small[0].wait()
    stream = hidden_v[...].astype(jnp.float32)
    own_sq = jnp.sum(stream * stream, axis=1, keepdims=True)
    sq_row = lax.broadcasted_iota(jnp.int32, (requests, HD), 0)
    sq_lane = lax.broadcasted_iota(jnp.int32, (requests, HD), 1)
    sq_diagonal = sq_row == sq_lane
    sq_buf[me] = jnp.sum(jnp.where(sq_diagonal, own_sq, 0.0), axis=0, keepdims=True)

    pl.semaphore_wait(barrier, n - 1)
    for mask in far_first:
        remote(
            sq_buf.at[me], sq_buf.at[me], send_sem.at[0], recv_sem.at[0], flipped(mask)
        ).start()

    own_place = pl.ds(pl.multiple_of(core * positions, positions), positions)
    kv_copy = pltpu.make_async_copy(
        kv_hbm.at[pl.ds(core * half_kv, half_kv)], kv_v.at[:, :, :, own_place], kv_sem.at[0]
    )
    kv_swap = remote(
        kv_hbm.at[pl.ds((1 - core) * half_kv, half_kv)],
        kv_v.at[:, :, :, own_place],
        kv_sem.at[1],
        kv_sem.at[2],
        partner,
    )
    kv_copy.start()
    kv_swap.start()

    for copy in small[1:]:
        copy.wait()
    gain = jnp.concatenate(
        [gain_v[k : k + 1, :].astype(jnp.float32) for k in range(width // HD)], axis=1
    )

    def tables(rows, first):
        row = lax.broadcasted_iota(jnp.int32, (rows, HD), 0) + first
        lane = lax.broadcasted_iota(jnp.int32, (rows, HD), 1)
        request = lax.rem(row, requests)
        length = jnp.zeros((rows, HD), jnp.float32)
        for b in range(requests):
            length = jnp.where(request == b, len_ref[b].astype(jnp.float32), length)
        angles = length * freq_v[...]
        sine = jnp.sin(angles)
        return row, jnp.cos(angles), jnp.where(lane < HD // 2, -sine, sine)

    member = lax.rem(chip, per_kv)
    _, q_cos, q_sin = tables(q_rows, 0)
    kv_row, kv_cos, kv_sin = tables(kv_rows, member * kv_rows)
    kv_cos = jnp.where(kv_row < requests, kv_cos, 1.0)
    kv_sin = jnp.where(kv_row < requests, kv_sin, 0.0)

    wkv_copy.wait()
    for copy in wq_copies:
        copy.wait()
    every(sq_buf, 0, n - 1).wait_recv()
    sq_total = jnp.sum(sq_buf[...], axis=0)
    squares = jnp.sum(jnp.where(sq_diagonal, sq_total, 0.0), axis=1, keepdims=True)
    normed = (stream * lax.rsqrt(squares / (width * n) + epsilon) * gain).astype(jnp.bfloat16)

    proj_kv = jnp.dot(normed, wkv_v[...], preferred_element_type=jnp.float32)
    for head in range(KVH):
        for t in range(per_kv):
            part, first = divmod(t * kv_rows, requests)
            lanes = (part * KVH + head) * HD
            kvp[head * per_kv + t] = proj_kv[first : first + kv_rows, lanes : lanes + HD]
    kv_pair = remote(
        kvp.at[pl.ds((1 - core) * chips, chips)],
        kv_d,
        pair_sem.at[0, STAGES],
        pair_sem.at[1, STAGES],
        partner,
    )
    kv_pair.start()

    def stage_slots(stage):
        return pl.ds(stage * in_stage, in_stage)

    def pair_copy(stage):
        return remote(
            q_other.at[stage_slots(stage)],
            q_d.at[stage_slots(stage)],
            pair_sem.at[0, stage],
            pair_sem.at[1, stage],
            partner,
        )

    def project(stage):
        for target, side in ((q_other, 0), (q_own, 1)):
            for step in range(stage * in_stage, (stage + 1) * in_stage):
                res = jnp.dot(normed, wq_v[2 * step + side], preferred_element_type=jnp.float32)
                for j in range(heads):
                    target[step, j * requests : (j + 1) * requests, :] = res[
                        :, j * HD : (j + 1) * HD
                    ]
        pair_copy(stage).start()

    def forward(stage):
        if stage == 0:
            kv_pair.wait_recv()
            kv_sum[...] = kvp[pl.ds(core * chips, chips)] + kv_d[...]
        pair_copy(stage).wait_recv()
        slots = slice(stage * in_stage, (stage + 1) * in_stage)
        q_own[slots] = q_own[slots] + q_d[slots]
        for step in range(stage * in_stage, (stage + 1) * in_stage):
            mask = chip_order[step]
            if mask:
                peer = flipped(2 * mask)
                remote(
                    q_own.at[step], q_in.at[chip], send_sem.at[1], recv_sem.at[1], peer
                ).start()
                remote(
                    kv_sum.at[peer // 2], kv_in.at[chip], send_sem.at[2], recv_sem.at[2], peer
                ).start()
            else:
                q_in[chip] = q_own[step]
                kv_in[chip] = kv_sum[chip]

    for stage in range(STAGES):
        project(stage)
        if stage >= 2:
            forward(stage - 2)
    forward(STAGES - 2)
    forward(STAGES - 1)
    wo_copy.start()

    every(q_in, 1, chips - 1).wait_recv()
    total = jnp.sum(q_in[...], axis=0)
    total = total * q_cos + pltpu.roll(total, HD // 2, 1) * q_sin
    rounded = total.astype(jnp.bfloat16)
    queries_own = rounded.astype(jnp.float32)
    q_buf[chip] = rounded
    for mask in chip_order[:-1]:
        remote(
            q_buf.at[chip], q_buf.at[chip], send_sem.at[3], recv_sem.at[3], flipped(2 * mask)
        ).start()

    every(kv_in, 2, chips - 1).wait_recv()
    kv_total = jnp.sum(kv_in[...], axis=0)
    kv_total = kv_total * kv_cos + pltpu.roll(kv_total, HD // 2, 1) * kv_sin
    kv_sib[member] = kv_total.astype(jnp.bfloat16).astype(jnp.float32)
    for step in range(1, per_kv):
        sibling = chip - member + lax.rem(member + step, per_kv)
        remote(
            kv_sib.at[member],
            kv_sib.at[member],
            send_sem.at[4],
            recv_sem.at[4],
            sibling * 2 + core,
        ).start()
    every(kv_sib, 4, per_kv - 1).wait_recv()
    for t in range(per_kv):
        kv_flat[t * kv_rows : (t + 1) * kv_rows, :] = kv_sib[t]
    for j in range(heads):
        k_rows[j * requests : (j + 1) * requests, :] = kv_flat[:requests, :]
        v_rows[j * requests : (j + 1) * requests, :] = kv_flat[requests:, :]
    new_score = jnp.sum(queries_own * k_rows[...], axis=1, keepdims=True) * score_scale
    lane = lax.broadcasted_iota(jnp.int32, (q_rows, HD), 1)
    row = lax.broadcasted_iota(jnp.int32, (q_rows, HD), 0)
    diagonal = lane == row
    shifted = lane == row + HD // 2
    new_lane = jnp.sum(jnp.where(diagonal, new_score, 0.0), axis=0, keepdims=True)

    all_rows = GROUP * requests
    row_req = lax.rem(lax.broadcasted_iota(jnp.int32, (all_rows, 1), 0), requests)
    column_pos = lax.broadcasted_iota(jnp.int32, (1, span), 1) + chip * span
    row_len = jnp.zeros((all_rows, 1), jnp.int32)
    for b in range(requests):
        row_len = jnp.where(row_req == b, len_ref[b], row_len)
    visible = column_pos < row_len

    kv_copy.wait()
    kv_swap.wait_recv()
    every(q_buf, 3, chips - 1).wait_recv()

    for h in range(half_kv):
        queries = q_buf[h * per_kv : (h + 1) * per_kv].reshape(all_rows, HD)
        places = [slab_ref[b, core * half_kv + h] for b in range(requests)]
        scores = None
        for b in range(requests):
            part = lax.dot_general(
                queries,
                kv_v[h, places[b], 0],
                (((1,), (1,)), ((), ())),
                preferred_element_type=jnp.float32,
            )
            scores = part if b == 0 else jnp.where(row_req == b, part, scores)
        scores = jnp.where(visible, scores * score_scale, lowest)
        top = jnp.max(scores, axis=1, keepdims=True)
        weights = jnp.where(visible, jnp.exp(scores - top), 0.0)
        weight_sum = jnp.sum(weights, axis=1, keepdims=True)
        weighted = jnp.zeros((all_rows, HD), jnp.float32)
        for b in range(requests):
            weighted = weighted + jnp.dot(
                jnp.where(row_req == b, weights, 0.0).astype(jnp.bfloat16),
                kv_v[h, places[b], 1],
                preferred_element_type=jnp.float32,
            )
        for t in range(per_kv):
            own = slice(t * q_rows, (t + 1) * q_rows)
            o_buf[h * per_kv + t] = weighted[own].astype(jnp.bfloat16)
            st_buf[h * per_kv + t] = jnp.sum(
                jnp.where(diagonal, top[own], 0.0) + jnp.where(shifted, weight_sum[own], 0.0),
                axis=0,
                keepdims=True,
            )

    for mask in chip_order[:-1]:
        peer = flipped(2 * mask)
        remote(
            st_buf.at[peer // 2], st_in.at[chip], send_sem.at[5], recv_sem.at[5], peer
        ).start()
        remote(o_buf.at[peer // 2], o_in.at[chip], send_sem.at[6], recv_sem.at[6], peer).start()
    o_in[chip] = o_buf[chip]
    st_in[chip] = st_buf[chip]

    every(st_in, 5, chips - 1).wait_recv()
    stats = st_in[...]
    top_lane = jnp.maximum(jnp.max(stats, axis=0), new_lane)
    factor = jnp.exp(jnp.minimum(stats - top_lane[None], 0.0))
    new_factor = jnp.exp(new_lane - top_lane)
    sums = jnp.concatenate([stats[:, :, HD // 2 :], stats[:, :, : HD // 2]], axis=2)
    denominator_lane = jnp.sum(factor * sums, axis=0) + new_factor

    def as_column(lanes):
        return jnp.sum(jnp.where(diagonal, lanes, 0.0), axis=1, keepdims=True)

    weighted = as_column(new_factor).astype(jnp.bfloat16).astype(jnp.float32) * v_rows[...]
    columns = jnp.sum(jnp.where(diagonal[None], factor, 0.0), axis=2, keepdims=True)
    denominator = as_column(denominator_lane)
    every(o_in, 6, chips - 1).wait_recv()
    weighted = weighted + jnp.sum(columns * o_in[...].astype(jnp.float32), axis=0)
    att_f[...] = weighted / denominator
    for j in range(heads):
        att_buf[me, :, j * HD : (j + 1) * HD] = att_f[
            j * requests : (j + 1) * requests, :
        ].astype(jnp.bfloat16)

    groups = [list(range(first, first + n // 4)) for first in range(0, n, n // 4)]
    group_of = {mask: k for k, group in enumerate(groups) for mask in group}
    for mask in far_first:
        remote(
            att_buf.at[me],
            att_buf.at[me],
            send_sem.at[7],
            att_sem.at[group_of[mask]],
            flipped(mask),
        ).start()

    wo_copy.wait()
    acc = stream
    for k, group in enumerate(groups):
        count = sum(mask > 0 for mask in group)
        part = att_buf.at[pl.ds(0, count)]
        remote(part, part, send_sem.at[7], att_sem.at[k], partner).wait_recv()
        for mask in group:
            source = flipped(mask)
            first = pl.multiple_of(block_of(source) * cols, cols)
            acc = acc + jnp.dot(
                att_buf[source],
                wo_v[pl.ds(first, cols), :],
                preferred_element_type=jnp.float32,
            )
    out_ref[...] = acc.astype(jnp.bfloat16)

    kv_swap.wait_send()
    kv_pair.wait_send()
    for stage in range(STAGES):
        pair_copy(stage).wait_send()
    every(sq_buf, 0, n - 1).wait_send()
    every(q_in, 1, chips - 1).wait_send()
    every(kv_in, 2, chips - 1).wait_send()
    every(q_buf, 3, chips - 1).wait_send()
    every(kv_sib, 4, per_kv - 1).wait_send()
    every(st_in, 5, chips - 1).wait_send()
    every(o_in, 6, chips - 1).wait_send()
    every(att_buf, 7, n - 1).wait_send()


def body(n, hidden_in, norm_gain, w_q, w_kv, w_o, kv_cache, lengths, slab_index):
    requests, width = hidden_in.shape
    chips = n // 2
    heads = KVH * GROUP // n
    cols = heads * HD
    q_rows = heads * requests
    per_kv = GROUP // heads
    kv_rows = 2 * requests // per_kv
    slabs, positions = kv_cache.shape[1], kv_cache.shape[3]

    exponent = -2.0 * (np.arange(HD) % (HD // 2)) / HD
    frequency = jnp.asarray((rope_base**exponent).astype(np.float32).reshape(1, HD))

    hbm = pl.BlockSpec(memory_space=pltpu.HBM)
    bf16, f32 = jnp.bfloat16, jnp.float32
    dma = pltpu.SemaphoreType.DMA
    return pl.pallas_call(
        functools.partial(step_kernel, n),
        out_shape=jax.ShapeDtypeStruct((requests, width), bf16),
        in_specs=[hbm] * 9,
        out_specs=pl.BlockSpec(memory_space=pltpu.VMEM),
        scratch_shapes=[
            pltpu.SMEM((requests, KVH), jnp.int32),
            pltpu.SMEM((requests,), jnp.int32),
            pltpu.VMEM((requests, width), bf16),
            pltpu.VMEM((width // HD, HD), bf16),
            pltpu.VMEM((1, HD), f32),
            pltpu.VMEM((n, width, cols), bf16),
            pltpu.VMEM(w_kv.shape, bf16),
            pltpu.VMEM(w_o.shape, bf16),
            pltpu.VMEM((KVH // 2, slabs, 2, 2 * positions, HD), bf16),
            pltpu.VMEM((n, 1, HD), f32),
            pltpu.VMEM((n, kv_rows, HD), f32),
            pltpu.VMEM((chips, kv_rows, HD), f32),
            pltpu.VMEM((chips, kv_rows, HD), f32),
            pltpu.VMEM((chips, kv_rows, HD), f32),
            pltpu.VMEM((per_kv, kv_rows, HD), f32),
            pltpu.VMEM((2 * requests, HD), f32),
            pltpu.VMEM((chips, q_rows, HD), f32),
            pltpu.VMEM((chips, q_rows, HD), f32),
            pltpu.VMEM((chips, q_rows, HD), f32),
            pltpu.VMEM((chips, q_rows, HD), f32),
            pltpu.VMEM((chips, q_rows, HD), bf16),
            pltpu.VMEM((q_rows, HD), f32),
            pltpu.VMEM((q_rows, HD), f32),
            pltpu.VMEM((chips, q_rows, HD), bf16),
            pltpu.VMEM((chips, q_rows, HD), bf16),
            pltpu.VMEM((chips, 1, HD), f32),
            pltpu.VMEM((chips, 1, HD), f32),
            pltpu.VMEM((q_rows, HD), f32),
            pltpu.VMEM((n, requests, cols), bf16),
            dma((5,)),
            dma((n,)),
            dma,
            dma,
            dma((3,)),
            dma((8,)),
            dma((7,)),
            dma((2, STAGES + 1)),
            dma((4,)),
        ],
        compiler_params=pltpu.CompilerParams(
            collective_id=0, has_side_effects=True, vmem_limit_bytes=44 * 1024 * 1024
        ),
    )(
        *(
            pltpu.with_memory_space_constraint(operand, pltpu.HBM)
            for operand in (
                slab_index.T,
                lengths,
                hidden_in,
                norm_gain.reshape(width // HD, HD),
                frequency,
                w_q,
                w_kv,
                w_o,
                kv_cache,
            )
        )
    )


def solution(mesh):
    placed = (
        P("groups", "tensor"),
        P("tensor"),
        P("tensor", None),
        P("tensor", None),
        P(None, "tensor"),
        P(None, "groups", None, "tensor", None),
        P("groups"),
        P(None, "groups"),
    )
    return jax.shard_map(
        functools.partial(body, mesh.shape["tensor"]),
        mesh=mesh,
        in_specs=placed,
        out_specs=P("groups", "tensor"),
        check_vma=False,
    )
```

time: 56 us -> 39 us (0.70)
  Pallas kernels: 49.7 us -> 38.3 us
  local copies, waits for them, and re-layouts: 5.12 us -> 0.6 us
  other arithmetic: 0.85 us -> 0 us
    pallas_call x1, Pallas kernels: 49.7 us -> 38.3 us  [body(): pl.pallas_call(functools.partial(step_kernel, n), out_shape=jax.ShapeDtyp...]
    unnamed x2 -> x1, local copies, waits for them, and re-layouts: 2.62 us -> 0.6 us
    reshape x1 -> x0, local copies, waits for them, and re-layouts: 1.26 us -> none  [body(): norm_gain.reshape(1, width)]
    concatenate x2 -> x0, local copies, waits for them, and re-layouts: 1.22 us -> none  [the longest x1 0.61 us: body(): jnp.concatenate([jnp.tile(cosine, (heads + 1, 1)), jnp.ones_like(cosine)]...]
    convert_element_type x1 -> x0, other arithmetic: 0.66 us -> none  [body(): angles = lengths.astype(jnp.float32)[:, None] * frequency]
where the time goes in v1:
time: 39 us; the launch traced here: 38.9 us
  Pallas kernels  38.3 us (98%)
  local copies, waits for them, and re-layouts  0.6 us (2%)
    pallas_call x1, Pallas kernels, body(): pl.pallas_call(functools.partial(step_kernel, n), out_shape=jax.ShapeDtyp...  38.3 us

profile of v1, /device:TPU:0, one launch (start us, length us, event | category | flops | bytes accessed | tf_op | source)
XLA Modules:
  0.0 38.9 jit_solution(8589164761459757125)
XLA Ops:
  0.0 38.3 %shard_map.91 = bf16[4,512]{1,0:T(4,128)(2,1)S(1)} custom-call(s32[4,8]{1,0:T(4,128)} %bitcast.2, s32[4]{0:T(128)} %len_hbm.1, bf16[4,512]{1,0:T(4,128)(2,1)} %hidden_hbm.1, bf16[4,128]{1,0:T(4,128)(2,1)} %bitcast.3, f32[1,128]{1,0:T(1,128)} %constant.2.clone.freq_hbm, bf16[512,16384]{1,0:T(8,128)(2,1)} %wq_hbm.1, bf16[512,2048]{1,0:T(8,128)(2,1)} %wkv_hbm.1, ...), custom_call_target="tpu_custom_call" | custom-call | tf_op jit(solution)/shard_map/pallas_call | solution.py:458
  38.3 0.6 %copy.11 = bf16[4,512]{1,0:T(4,128)(2,1)} copy(bf16[4,512]{1,0:T(4,128)(2,1)S(1)} %shard_map.91) | data formatting | bytes 8192
